TPU v7x, 256 devices: a whole 4x4x8 slice. The times are simulated.
256 devices in a mesh: samp: 32 (over z, y_hi, core), snp: 8 (over y_lo, x).
Axes of the slice: x: 4, y: 4 (y_hi: 2, y_lo: 2; y = y_hi * 2 + y_lo), z: 8, core: 2. Of those that a mesh axis runs over, the one named last changes fastest.
Arguments:
- genotypes: float32 [8192, 8192], P('samp', 'snp'), may hold values from 0 to 2, as said below
- observed: int32 [8192, 8192], P('samp', 'snp'), may hold values from 0 to 1
Outputs:
- relation: float32 [32, 8, 32, 8192], P(None, 'snp', None, 'samp')
Inputs may be any that keep to these rules, and one draw needn't show every extreme that they name: `genotypes`: dosages are real numbers between 0 and 2.
All inputs are finite; a program needn't handle non-finite values.
Results may differ from a plain program's by a relative error of at most 0.00061.
Values may be sent and summed in bfloat16 or wider, within the bound.
No kernel may reach another device: no remote copies, remote signals or barrier semaphores. Data moves between devices by JAX's collectives and lax.ppermute only.
A program may use at most 128 MiB of HBM per device.

v0:
```python
import jax
import jax.numpy as jnp
from jax import lax
from jax.sharding import PartitionSpec as P

var_floor = 0.1


def from_everyone(x, axis):
    devices = lax.axis_size(axis)
    return lax.all_to_all(jnp.broadcast_to(x[None], (devices, *x.shape)), axis, 0, 0, tiled=True)


def taken_together(x, axis):
    everything = from_everyone(x, axis)
    return jnp.sum(everything, axis=0)


def together(arrays, axis):
    ends = [0]
    for a in arrays:
        ends.append(ends[-1] + a.size)
    total = taken_together(jnp.concatenate([a.ravel() for a in arrays]), axis)
    return tuple((total[b:e].reshape(a.shape) for a, b, e in zip(arrays, ends, ends[1:])))


def body(genotypes, observed):
    row_count, snp_count = genotypes.shape
    present = observed.astype(jnp.float32)
    alt_local = jnp.sum(present * genotypes, axis=0)
    call_local = jnp.sum(present, axis=0)
    alt_sum, call_sum = together((alt_local, call_local), "samp")
    frequency = alt_sum / (2.0 * jnp.maximum(call_sum, 1.0))
    variance = jnp.maximum(2.0 * frequency * (1.0 - frequency), var_floor)
    scaled = (present * (genotypes - 2.0 * frequency) * lax.rsqrt(variance)).astype(jnp.bfloat16)
    shards = lax.axis_size("samp")
    groups = lax.axis_size("snp")
    tile_rows = row_count // groups
    total_snps = snp_count * groups
    own_panel = lax.all_gather(scaled, "snp", axis=1, tiled=True)
    blocks = scaled.reshape(groups, tile_rows, snp_count)
    owned_rows = lax.all_to_all(blocks, "snp", split_axis=0, concat_axis=2, tiled=True)
    owned_rows = owned_rows.reshape(tile_rows, total_snps)
    summed = lax.dot_general(
        lax.all_gather(owned_rows, "samp", axis=0, tiled=True),
        own_panel,
        (((1,), (1,)), ((), ())),
        preferred_element_type=jnp.float32,
    )
    summed = summed.reshape(shards, 1, tile_rows, row_count)
    return summed / total_snps


def solution(mesh):
    return jax.shard_map(
        body,
        mesh=mesh,
        in_specs=(P("samp", "snp"), P("samp", "snp")),
        out_specs=P(None, "snp", None, "samp"),
        check_vma=False,
    )
```

profile of v0, /device:TPU:1, one launch (start us, length us, event | category | flops | bytes accessed | tf_op | source)
XLA Modules:
  0.0 245.6 jit_solution(18037408167674693054)
XLA Ops:
  6.5 0.0 all-gather.5.cloned.1.call-start
  6.5 1.8 multiply_reduce_fusion
  8.3 0.1 broadcast_in_dim.2
  8.5 25.5 %all_to_all.21 = f32[32,1,2048]{2,1,0:T(1,128)S(1)} all-to-all(f32[32,1,2048]{2,1,0:T(1,128)S(1)} %broadcast_in_dim.2), channel_id=1, replica_groups=mesh['samp'=32,'snp'=8] {'samp'}, dimensions={0} | all-to-all | bytes 524288 | tf_op jit(solution)/shard_map/all_to_all | solution.py:11
  33.9 0.2 reduce_sum.29
  34.1 2.6 %multiply_convert_fusion = bf16[256,1024]{1,0:T(8,128)(2,1)} fusion(f32[256,1024]{1,0:T(8,128)} %param.2, s32[256,1024]{1,0:T(8,128)} %param.3, f32[1024]{0:T(1024)S(1)} %get-tuple-element.8, f32[1024]{0:T(1024)S(1)} %get-tuple-element.7), kind=kLoop, calls=%fused_computation.1 | loop fusion | flops 1310720 | bytes 2629632 | tf_op jit(solution)/shard_map/convert_element_type | solution.py:35
  36.7 0.0 all-gather.5.cloned.1.call-update
  36.7 0.0 all-gather.3.cloned.1.call-start
  36.8 15.4 %all_to_all.22 = bf16[8,32,1024]{2,1,0:T(8,128)(2,1)S(1)} all-to-all(bf16[8,32,1024]{2,1,0:T(8,128)(2,1)} %bitcast.14), channel_id=1, replica_groups=mesh['samp'=32,'snp'=8] {'snp'}, dimensions={0} | all-to-all | bytes 1048576 | tf_op jit(solution)/shard_map/all_to_all | solution.py:42
  52.1 0.8 copy.16
  53.0 0.0 all-gather.3.cloned.1.call-update
  53.0 38.4 %all-gather.5.cloned.1.call-done = bf16[256,8192]{1,0:T(8,128)(2,1)} async-done(((bf16[256,1024]{1,0:T(8,128)(2,1)}), bf16[256,8192]{1,0:T(8,128)(2,1)}) %all-gather.5.cloned.1.call-update) | async-done | bytes 4194320 | tf_op jit(solution)/shard_map/all_gather | solution.py:40
  91.4 135.0 %all-gather.3.cloned.1.call-done = bf16[1024,8192]{1,0:T(8,128)(2,1)} async-done(((bf16[32,8192]{1,0:T(8,128)(2,1)}), bf16[1024,8192]{1,0:T(8,128)(2,1)}) %all-gather.3.cloned.1.call-update) | async-done | bytes 16777232 | tf_op jit(solution)/shard_map/all_gather | solution.py:45
  226.3 12.5 %convolution_multiply_fusion = f32[1024,256]{1,0:T(8,128)} fusion(bf16[1024,8192]{1,0:T(8,128)(2,1)} %all-gather.3.cloned.1.call-done, bf16[256,8192]{1,0:T(8,128)(2,1)} %all-gather.5.cloned.1.call-done), kind=kOutput, calls=%fused_computation | convolution fusion | flops 4295229440 | bytes 22020096 | tf_op jit(solution)/shard_map/dot_general | solution.py:44
  (2 shorter events, 0.0 us)
Async XLA Ops:
  6.5 84.8 %all-gather.5.cloned.1.call-start = ((), (), s32[]{:S(2)}) async-start(), calls=%async_computation.3 | async-start | bytes 4718592 | tf_op jit(solution)/shard_map/all_gather | solution.py:40
  36.7 189.6 %all-gather.3.cloned.1.call-start = ((), (), s32[]{:S(2)}) async-start(), calls=%async_computation.2 | async-start | bytes 17301504 | tf_op jit(solution)/shard_map/all_gather | solution.py:45
Sparse Core Ops, SparseCore 0:
  36.8 54.4 all-gather.4
  94.1 132.1 all-gather.2
where the time goes:
time: 246 us
  waiting for transfers between devices  173 us (70%)
  blocking collectives  40.8 us (17%)
  between operations  13.4 us (5%)
  matrix products  12.5 us (5%)
  other arithmetic  4.52 us (2%)
    all_gather x1, waiting for transfers between devices, body(): lax.all_gather(owned_rows, 'samp', axis=0, tiled=True)  135 us
    all_gather x1, waiting for transfers between devices, body(): own_panel = lax.all_gather(scaled, 'snp', axis=1, tiled=True)  38.4 us
    all_to_all x1, blocking collectives, from_everyone(): lax.all_to_all(jnp.broadcast_to(x[None], (devices, *x.shape)), axis, 0, 0...  25.5 us
    all_to_all x1, blocking collectives, body(): lax.all_to_all(blocks, 'snp', split_axis=0, concat_axis=2, tiled=True)  15.4 us
    dot_general x1, matrix products, body(): lax.dot_general(lax.all_gather(owned_rows, 'samp', axis=0, tiled=True), o...  12.5 us
  transfers between devices with their start and end apart: 2, of which 2 were waited for; matrix products, arithmetic and copies ran while one was open for 0% of the time, Pallas kernels for 0%

commit v1 on v0

--- a/solution.py
+++ b/solution.py
@@ -37,7 +37,9 @@
     groups = lax.axis_size("snp")
     tile_rows = row_count // groups
     total_snps = snp_count * groups
-    own_panel = lax.all_gather(scaled, "snp", axis=1, tiled=True)
+    own_panel = jnp.concatenate(
+        lax.all_to_all(jnp.stack([scaled] * lax.axis_size("snp")), "snp", 0, 0), axis=1
+    )
     blocks = scaled.reshape(groups, tile_rows, snp_count)
     owned_rows = lax.all_to_all(blocks, "snp", split_axis=0, concat_axis=2, tiled=True)
     owned_rows = owned_rows.reshape(tile_rows, total_snps)

time: 246 us -> 237 us (0.963)
  waiting for transfers between devices: 173 us -> 100 us
  blocking collectives: 40.8 us -> 93.1 us
  local copies, waits for them, and re-layouts: 0.97 us -> 13.2 us
    all_to_all x0 -> x1, blocking collectives: none -> 54.2 us  [body(): lax.all_to_all(jnp.stack([scaled] * lax.axis_size('snp')), 'snp', 0, 0)]
    all_gather x1 -> x0, waiting for transfers between devices: 38.4 us -> none  [body(): own_panel = lax.all_gather(scaled, 'snp', axis=1, tiled=True)]
    all_gather x1, waiting for transfers between devices: 135 us -> 100 us  [body(): lax.all_gather(owned_rows, 'samp', axis=0, tiled=True)]
    reshape x0 -> x2, local copies, waits for them, and re-layouts: none -> 11.7 us  [body(): jnp.concatenate(lax.all_to_all(jnp.stack([scaled] * lax.axis_size('snp'))...]
  transfers between devices with their start and end apart: 2 -> 1, of which waited for: 2 -> 1; matrix products, arithmetic and copies ran while one was open for 0% -> 5% of each run, Pallas kernels for 0% -> 0%
where the time goes in v1:
time: 237 us; the launch traced here: 236 us
  waiting for transfers between devices  100 us (42%)
  blocking collectives  93.1 us (39%)
  between operations  13.4 us (6%)
  local copies, waits for them, and re-layouts  13.2 us (6%)
  matrix products  12.5 us (5%)
  other arithmetic  3.72 us (2%)
    all_gather x1, waiting for transfers between devices, body(): lax.all_gather(owned_rows, 'samp', axis=0, tiled=True)  100 us
    all_to_all x1, blocking collectives, body(): lax.all_to_all(jnp.stack([scaled] * lax.axis_size('snp')), 'snp', 0, 0)  54.2 us
    all_to_all x1, blocking collectives, from_everyone(): lax.all_to_all(jnp.broadcast_to(x[None], (devices, *x.shape)), axis, 0, 0...  25.5 us
    all_to_all x1, blocking collectives, body(): lax.all_to_all(blocks, 'snp', split_axis=0, concat_axis=2, tiled=True)  13.4 us
    dot_general x1, matrix products, body(): lax.dot_general(lax.all_gather(owned_rows, 'samp', axis=0, tiled=True), o...  12.5 us
    reshape x2, local copies, waits for them, and re-layouts, body(): jnp.concatenate(lax.all_to_all(jnp.stack([scaled] * lax.axis_size('snp'))...  11.7 us
  transfers between devices with their start and end apart: 1, of which 1 were waited for; matrix products, arithmetic and copies ran while one was open for 5% of the time, Pallas kernels for 0%

profile of v1, /device:TPU:1, one launch (start us, length us, event | category | flops | bytes accessed | tf_op | source)
XLA Modules:
  0.0 236.1 jit_solution(14681781119131452409)
XLA Ops:
  6.5 0.0 all-gather.2.cloned.1.call-start
  6.5 1.8 multiply_reduce_fusion
  8.3 0.1 broadcast_in_dim.2
  8.5 25.5 %all_to_all.26 = f32[32,1,2048]{2,1,0:T(1,128)S(1)} all-to-all(f32[32,1,2048]{2,1,0:T(1,128)S(1)} %broadcast_in_dim.2), channel_id=1, replica_groups=mesh['samp'=32,'snp'=8] {'samp'}, dimensions={0} | all-to-all | bytes 524288 | tf_op jit(solution)/shard_map/all_to_all | solution.py:11
  33.9 0.2 reduce_sum.29
  34.1 1.8 multiply_convert_fusion
  35.9 13.4 %all_to_all.27 = bf16[8,32,1024]{2,1,0:T(8,128)(2,1)S(1)} all-to-all(bf16[8,32,1024]{2,1,0:T(8,128)(2,1)S(1)} %bitcast.18), channel_id=1, replica_groups=mesh['samp'=32,'snp'=8] {'snp'}, dimensions={0} | all-to-all | bytes 1048576 | tf_op jit(solution)/shard_map/all_to_all | solution.py:44
  49.3 0.8 copy.18
  50.1 0.0 all-gather.2.cloned.1.call-update
  50.1 0.5 stack.2
  50.7 54.2 %all_to_all.28 = bf16[8,256,1024]{2,1,0:T(8,128)(2,1)S(1)} all-to-all(bf16[8,256,1024]{2,1,0:T(8,128)(2,1)S(1)} %stack.2), channel_id=1, replica_groups=mesh['samp'=32,'snp'=8] {'snp'}, dimensions={0} | all-to-all | bytes 8388608 | tf_op jit(solution)/shard_map/all_to_all | solution.py:41
  104.9 4.3 %copy.13 = bf16[256,8,1024]{2,1,0:T(8,128)(2,1)} copy(bf16[256,8,1024]{2,0,1:T(8,128)(2,1)S(1)} %bitcast.17) | data formatting | bytes 8388608 | tf_op jit(solution)/shard_map/reshape | solution.py:40
  109.2 7.4 %reshape.31 = bf16[256,8192,1]{1,0,2:T(8,128)(2,1)} reshape(bf16[256,8,1024]{2,1,0:T(8,128)(2,1)} %copy.13) | data formatting | bytes 8388608 | tf_op jit(solution)/shard_map/reshape | solution.py:40
  116.6 100.2 %all-gather.2.cloned.1.call-done = bf16[1024,8192]{1,0:T(8,128)(2,1)} async-done(((bf16[32,8192]{1,0:T(8,128)(2,1)}), bf16[1024,8192]{1,0:T(8,128)(2,1)}) %all-gather.2.cloned.1.call-update) | async-done | bytes 16777232 | tf_op jit(solution)/shard_map/all_gather | solution.py:47
  216.8 12.5 %fusion = f32[32,1,32,256]{3,2,1,0:T(8,128)} fusion(bf16[32,32,8192]{2,1,0:T(8,128)(2,1)} %bitcast.21, bf16[256,8192,1]{1,0,2:T(8,128)(2,1)} %reshape.31), kind=kOutput, calls=%fused_computation.1 | convolution fusion | flops 4295229440 | bytes 22020096 | tf_op jit(solution)/shard_map/dot_general | solution.py:46
  (2 shorter events, 0.0 us)
Async XLA Ops:
  6.5 210.3 %all-gather.2.cloned.1.call-start = ((), (), s32[]{:S(2)}) async-start(), calls=%async_computation.3 | async-start | bytes 17301504 | tf_op jit(solution)/shard_map/all_gather | solution.py:47
Sparse Core Ops, SparseCore 0:
  50.3 166.4 all-gather.1
